TPU v7x, 32 devices: a whole 2x2x4 slice. The times are simulated.
32 devices in a mesh: wide: 8 (over z, core), narrow: 4 (over y, x).
Axes of the slice: x: 2, y: 2, z: 4, core: 2. Of those that a mesh axis runs over, the one named last changes fastest.
Arguments:
- points: float32 [8192, 128], P(('wide', 'narrow')), may hold values from -6 to 6
- targets: float32 [16, 8192], P(None, ('wide', 'narrow')), may hold values from -6 to 6
- start: float32 [16, 8192], P(None, ('wide', 'narrow')), may hold values from -6 to 6
- interp: float32 [8192, 128], P(('wide', 'narrow')), may hold values from -0.375 to 0.375
- skel_points: float32 [1024, 128], P('wide'), may hold values from -6 to 6
- near_leaves: int32 [64, 8], P(('wide', 'narrow')), may hold values from 0 to 7, as said below
- near_count: int32 [64], P(('wide', 'narrow')), may hold values from 1 to 8
Outputs:
- weights: float32 [16, 8192], P(None, ('wide', 'narrow'))
- residual: float32 [16, 8192], P(None, ('wide', 'narrow'))
Inputs may be any that keep to these rules, and one draw needn't show every extreme that they name: `near_leaves`: each row names 8 different leaves of the row's own subtree.
All inputs are finite; a program needn't handle non-finite values.
Results may differ from a plain program's by a relative error of at most 0.0003.
Values sent between devices are 32-bit elements; how exact they have to be, the bound alone decides.
No kernel may reach another device: no remote copies, remote signals or barrier semaphores. Data moves between devices by JAX's collectives and lax.ppermute only.
A program may use at most 64 MiB of HBM per device.

v0:
```python
import math
import jax
import jax.numpy as jnp
from jax import lax
from jax.sharding import PartitionSpec as P

ITERS = 2
ridge_shift = 1.0
step_size = 0.05
kernel_rate = 2.0
highest = lax.Precision.HIGHEST


def kernel(left_points, right_points, features):
    cross_prod = jnp.dot(
        left_points, right_points.T, precision=highest, preferred_element_type=jnp.float32
    )
    left_sq = jnp.sum(left_points * left_points, axis=1)
    right_sq = jnp.sum(right_points * right_points, axis=1)
    return jnp.exp(
        -(kernel_rate / features) * (left_sq[:, None] + right_sq[None, :] - 2.0 * cross_prod)
    )


def far_block(row_blocks, skeleton, columns, features):

    def row_group(block_points):
        kernel_vals = kernel(block_points, skeleton, features)
        return jnp.einsum("rs,ps->rp", columns, kernel_vals, precision=highest)

    pieces_out = lax.map(row_group, row_blocks)
    return jnp.transpose(pieces_out, (1, 0, 2)).reshape(columns.shape[0], -1)


def on_device(points, targets, start, interp, skel_points, near_leaves, near_count):
    leaf_dev, near_slots = near_leaves.shape
    row_total, features = points.shape
    leaf_size = row_total // leaf_dev
    rhs_count = targets.shape[0]
    skel_rank = interp.shape[1]
    block_rows = math.gcd(row_total, 512)
    row_blocks = points.reshape(row_total // block_rows, block_rows, features)
    own_blocks = points.reshape(leaf_dev, leaf_size, features)
    subtree = lax.all_gather(points, "narrow", axis=0, tiled=True).reshape(-1, leaf_size, features)
    neighbours = subtree[near_leaves]
    cross_prod = jnp.einsum("ipd,ikqd->ikpq", own_blocks, neighbours, precision=highest)
    own_sq = jnp.sum(own_blocks * own_blocks, axis=-1)
    near_sq = jnp.sum(neighbours * neighbours, axis=-1)
    live_mask = (jnp.arange(near_slots, dtype=jnp.int32)[None, :] < near_count[:, None]).astype(
        jnp.float32
    )
    distance = own_sq[:, None, :, None] + near_sq[:, :, None, :] - 2.0 * cross_prod
    near_kern = jnp.exp(-(kernel_rate / features) * distance) * live_mask[:, :, None, None]
    group_index = lax.axis_index("wide")
    weights = start
    residual = targets
    for iteration in range(ITERS):
        gathered = lax.all_gather(weights, "narrow", axis=1, tiled=True).reshape(
            rhs_count, -1, leaf_size
        )
        picked = gathered[:, near_leaves]
        near_term = jnp.einsum("ikpq,rikq->rip", near_kern, picked, precision=highest).reshape(
            rhs_count, row_total
        )
        node_local = jnp.dot(weights, interp, precision=highest, preferred_element_type=jnp.float32)
        summed = lax.psum(node_local, "narrow")
        skel_table = lax.all_gather(summed, "wide", axis=1, tiled=True)
        owner_node = jnp.arange(skel_table.shape[1], dtype=jnp.int32) // skel_rank
        skel_table = jnp.where((owner_node == group_index)[None, :], jnp.float32(0.0), skel_table)
        far_term = far_block(
            row_blocks,
            lax.all_gather(skel_points, "wide", axis=0, tiled=True),
            skel_table,
            features,
        )
        residual = targets - (ridge_shift * weights + (near_term + far_term))
        weights = weights + step_size * residual
    return (weights, residual)


def solution(mesh):
    in_specs = (
        P(("wide", "narrow"), None),
        P(None, ("wide", "narrow")),
        P(None, ("wide", "narrow")),
        P(("wide", "narrow"), None),
        P("wide", None),
        P(("wide", "narrow"), None),
        P(("wide", "narrow")),
    )
    out_specs = (P(None, ("wide", "narrow")), P(None, ("wide", "narrow")))
    return jax.shard_map(
        on_device, mesh=mesh, in_specs=in_specs, out_specs=out_specs, check_vma=False
    )
```

profile of v0, /device:TPU:0, one launch (start us, length us, event | category | flops | bytes accessed | tf_op | source)
XLA Modules:
  0.0 100.6 jit_solution(13071996611529464808)
XLA Ops:
  0.6 0.7 compare_select_fusion
  1.5 11.9 %all_gather.20 = f32[1024,128]{1,0:T(8,128)S(1)} all-gather(f32[256,128]{1,0:T(8,128)} %param.7), channel_id=1, replica_groups=mesh['wide'=8,'narrow'=4] {'narrow'}, dimensions={0}, use_global_device_ids=true | all-gather | bytes 655360 | tf_op jit(solution)/shard_map/all_gather | solution.py:44
  13.3 0.6 gather_fusion.1
  14.0 0.3 multiply_reduce_fusion
  14.3 0.5 copy-done.1
  15.0 0.6 copy-done.5
  15.7 1.2 %fusion.7 = f32[2,8,128,128]{2,3,1,0:T(8,128)S(1)} fusion(f32[2,8,128,128]{3,2,1,0:T(8,128)S(1)} %bitcast.65, f32[2,128,128,1]{2,1,3,0:T(8,128)S(1)} %bitcast.67, f32[2,8]{1,0:T(2,128)S(1)} %compare_convert_fusion, f32[2,8,128]{2,1,0:T(8,128)S(1)} %multiply_reduce_fusion, f32[2,128]{1,0:T(2,128)S(1)} %bitcast.70), kind=kOutput, calls=%fused_computation.12 | convolution fusion | flops 403963904 | bytes 2237504 | tf_op jit(solution)/shard_map/ipd,ikqd->ikpq/dot_general | solution.py:46
  16.9 7.9 %all_gather.19 = f32[16,1024]{1,0:T(8,128)S(1)} all-gather(f32[16,256]{1,0:T(8,128)S(1)} %copy-done.2), channel_id=1, replica_groups=mesh['wide'=8,'narrow'=4] {'narrow'}, dimensions={1}, use_global_device_ids=true | all-gather | bytes 81920 | tf_op jit(solution)/shard_map/all_gather | solution.py:58
  24.8 0.6 gather_fusion
  25.4 0.6 convolution_bitcast_fusion.1
  26.0 0.2 copy-done.4
  26.2 15.2 %all_gather.22 = f32[1024,128]{1,0:T(8,128)S(1)} all-gather(f32[128,128]{1,0:T(8,128)S(1)} %copy-done.4), channel_id=1, replica_groups=mesh['wide'=8,'narrow'=4] {'wide'}, dimensions={0}, use_global_device_ids=true | all-gather | bytes 589824 | tf_op jit(solution)/shard_map/all_gather | solution.py:72
  41.4 0.2 multiply_reduce_fusion.1
  41.6 1.2 %fusion.2 = f32[256,1024]{1,0:T(8,128)S(1)} fusion(f32[256,128]{1,0:T(8,128)S(1)} %copy-done.1, f32[1024,128]{1,0:T(8,128)S(1)} %all_gather.22, f32[1024]{0:T(1024)S(1)} %multiply_reduce_fusion.1, f32[256]{0:T(256)S(1)} %multiply_reduce_fusion.2), kind=kOutput, calls=%fused_computation.6 | convolution fusion | flops 403701760 | bytes 1709056 | tf_op jit(solution)/shard_map/while/body/eval_jaxpr/dot_general | solution.py:15
  43.0 9.1 %psum.14 = f32[16,128]{1,0:T(8,128)S(1)} all-reduce(f32[16,128]{1,0:T(8,128)S(1)} %fusion.26), channel_id=1, replica_groups=mesh['wide'=8,'narrow'=4] {'narrow'}, use_global_device_ids=true, to_apply=%region_2.0 | all-reduce | flops 2048 | bytes 16384 | tf_op jit(solution)/shard_map/psum | solution.py:66
  52.1 14.0 %all_gather.21 = f32[16,1024]{1,0:T(8,128)S(1)} all-gather(f32[16,128]{1,0:T(8,128)S(1)} %psum.14), channel_id=1, replica_groups=mesh['wide'=8,'narrow'=4] {'wide'}, dimensions={1}, use_global_device_ids=true | all-gather | bytes 73728 | tf_op jit(solution)/shard_map/all_gather | solution.py:67
  66.1 0.9 fusion.13
  67.0 7.6 %all_gather.23 = f32[16,1024]{1,0:T(8,128)S(1)} all-gather(f32[16,256]{1,0:T(8,128)S(1)} %fusion.13), channel_id=1, replica_groups=mesh['wide'=8,'narrow'=4] {'narrow'}, dimensions={1}, use_global_device_ids=true | all-gather | bytes 81920 | tf_op jit(solution)/shard_map/all_gather | solution.py:58
  74.6 0.6 gather_fusion.2
  75.2 0.6 convolution_bitcast_fusion
  75.8 0.2 fusion.27
  76.0 9.1 %psum.15 = f32[16,128]{1,0:T(8,128)S(1)} all-reduce(f32[16,128]{1,0:T(8,128)S(1)} %fusion.27), channel_id=1, replica_groups=mesh['wide'=8,'narrow'=4] {'narrow'}, use_global_device_ids=true, to_apply=%region_4.5 | all-reduce | flops 2048 | bytes 16384 | tf_op jit(solution)/shard_map/psum | solution.py:66
  85.1 14.0 %all_gather.24 = f32[16,1024]{1,0:T(8,128)S(1)} all-gather(f32[16,128]{1,0:T(8,128)S(1)} %psum.15), channel_id=1, replica_groups=mesh['wide'=8,'narrow'=4] {'wide'}, dimensions={1}, use_global_device_ids=true | all-gather | bytes 73728 | tf_op jit(solution)/shard_map/all_gather | solution.py:67
  99.0 1.5 %multiply_add_fusion = (f32[16,256]{1,0:T(8,128)}, f32[16,256]{1,0:T(8,128)}) fusion(f32[16,256]{1,0:T(8,128)S(1)} %fusion.13, f32[16,256]{1,0:T(8,128)S(1)} %copy-done.3, f32[256,1024]{1,0:T(8,128)S(1)} %fusion.2, f32[16,1024]{1,0:T(8,128)S(1)} %all_gather.24, pred[1024]{0:T(1024)(128)(4,1)S(1)} %fusion.20, f32[2,2,8,128]{3,2,1,0:T(8,128)S(1)} %convolution_bitcast_fusion), kind=kOutput, calls=%fused_computation.34 | convolution fusion | flops 50368512 | bytes 1197056 | tf_op jit(solution)/shard_map/while/body/eval_jaxpr/rs,ps->rp/dot_general | solution.py:29
  (17 shorter events, 0.5 us)
Async XLA Ops:
  0.6 42.2 %copy-start = (f32[256,128]{1,0:T(8,128)S(1)}, f32[256,128]{1,0:T(8,128)}, u32[]{:S(2)}) copy-start(f32[256,128]{1,0:T(8,128)} %param.10) | copy-start | bytes 393220
  13.9 0.9 copy-start.1
  15.0 0.7 copy-start.5
  15.7 1.2 %copy-start.2 = (f32[16,256]{1,0:T(8,128)S(1)}, f32[16,256]{1,0:T(8,128)}, u32[]{:S(2)}) copy-start(f32[16,256]{1,0:T(8,128)} %param.9) | copy-start | bytes 49156
  25.4 0.8 copy-start.4
  52.1 14.0 %copy-start.3 = (f32[16,256]{1,0:T(8,128)S(1)}, f32[16,256]{1,0:T(8,128)}, u32[]{:S(2)}) copy-start(f32[16,256]{1,0:T(8,128)} %param.8) | copy-start | bytes 49156
where the time goes:
time: 101 us
  blocking collectives  88.6 us (88%)
  matrix products  6.43 us (6%)
  local copies, waits for them, and re-layouts  3.27 us (3%)
  other arithmetic  1.46 us (1%)
    all_gather x2, blocking collectives, on_device(): skel_table = lax.all_gather(summed, 'wide', axis=1, tiled=True)  27.9 us
    psum x2, blocking collectives, on_device(): summed = lax.psum(node_local, 'narrow')  18.2 us
    all_gather x2, blocking collectives, on_device(): lax.all_gather(weights, 'narrow', axis=1, tiled=True)  15.5 us
    all_gather x1, blocking collectives, on_device(): lax.all_gather(skel_points, 'wide', axis=0, tiled=True)  15.2 us
    all_gather x1, blocking collectives, on_device(): lax.all_gather(points, 'narrow', axis=0, tiled=True)  11.9 us
    dot_general x2, matrix products, row_group(): return jnp.einsum('rs,ps->rp', columns, kernel_vals, precision=highest)  2.48 us

commit v1 on v0

--- a/solution.py
+++ b/solution.py
@@ -63,7 +63,14 @@
             rhs_count, row_total
         )
         node_local = jnp.dot(weights, interp, precision=highest, preferred_element_type=jnp.float32)
-        summed = lax.psum(node_local, "narrow")
+        wide_n = jax.lax.axis_size("narrow")
+        summed, tile_out = (node_local, 0)
+        while 1 << tile_out < wide_n:
+            formed = jax.lax.ppermute(
+                summed, "narrow", [(w, w ^ 1 << tile_out) for w in range(wide_n)]
+            )
+            summed = summed + formed
+            tile_out = tile_out + 1
         skel_table = lax.all_gather(summed, "wide", axis=1, tiled=True)
         owner_node = jnp.arange(skel_table.shape[1], dtype=jnp.int32) // skel_rank
         skel_table = jnp.where((owner_node == group_index)[None, :], jnp.float32(0.0), skel_table)

time: 101 us -> 97.8 us (0.968)
  blocking collectives: 88.6 us -> 69.1 us
  waiting for transfers between devices: 0 us -> 7.27 us
  starting transfers between devices: 0 us -> 5.35 us
  matrix products: 6.43 us -> 7.75 us
  other arithmetic: 1.46 us -> 2.62 us
  local copies, waits for them, and re-layouts: 3.27 us -> 4.38 us
    psum x2 -> x0, blocking collectives: 18.2 us -> none  [on_device(): summed = lax.psum(node_local, 'narrow')]
    ppermute x0 -> x4, waiting for transfers between devices: none -> 7.27 us  [on_device(): jax.lax.ppermute(summed, 'narrow', [(w, w ^ 1 << tile_out) for w in range...]
    ppermute x0 -> x4, starting transfers between devices: none -> 5.35 us  [on_device(): jax.lax.ppermute(summed, 'narrow', [(w, w ^ 1 << tile_out) for w in range...]
    all_gather x1, blocking collectives: 11.9 us -> 10.2 us  [on_device(): lax.all_gather(points, 'narrow', axis=0, tiled=True)]
    dot_general x2, matrix products: 0.35 us -> 1.67 us  [on_device(): jnp.dot(weights, interp, precision=highest, preferred_element_type=jnp.fl...]
    unnamed x12 -> x24, local copies, waits for them, and re-layouts: 1.43 us -> 2.42 us
  transfers between devices with their start and end apart: 0 -> 4, of which waited for: 0 -> 3; matrix products, arithmetic and copies ran while one was open for 0% -> 8% of each run, Pallas kernels for 0% -> 0%
where the time goes in v1:
time: 97.8 us; the launch traced here: 97.3 us
  blocking collectives  69.1 us (71%)
  matrix products  7.75 us (8%)
  waiting for transfers between devices  7.27 us (7%)
  starting transfers between devices  5.35 us (5%)
  local copies, waits for them, and re-layouts  4.38 us (4%)
  other arithmetic  2.62 us (3%)
    all_gather x2, blocking collectives, on_device(): skel_table = lax.all_gather(summed, 'wide', axis=1, tiled=True)  28 us
    all_gather x2, blocking collectives, on_device(): lax.all_gather(weights, 'narrow', axis=1, tiled=True)  15.6 us
    all_gather x1, blocking collectives, on_device(): lax.all_gather(skel_points, 'wide', axis=0, tiled=True)  15.2 us
    all_gather x1, blocking collectives, on_device(): lax.all_gather(points, 'narrow', axis=0, tiled=True)  10.2 us
    ppermute x4, waiting for transfers between devices, on_device(): jax.lax.ppermute(summed, 'narrow', [(w, w ^ 1 << tile_out) for w in range...  7.27 us
    ppermute x4, starting transfers between devices, on_device(): jax.lax.ppermute(summed, 'narrow', [(w, w ^ 1 << tile_out) for w in range...  5.35 us
    dot_general x2, matrix products, row_group(): return jnp.einsum('rs,ps->rp', columns, kernel_vals, precision=highest)  2.48 us
    unnamed x24, local copies, waits for them, and re-layouts  2.42 us
  transfers between devices with their start and end apart: 4, of which 3 were waited for; matrix products, arithmetic and copies ran while one was open for 8% of the time, Pallas kernels for 0%

profile of v1, /device:TPU:0, one launch (start us, length us, event | category | flops | bytes accessed | tf_op | source)
XLA Modules:
  0.0 97.3 jit_solution(1232495998820689823)
XLA Ops:
  0.7 0.9 copy-done
  1.5 1.5 %fusion.26 = f32[16,128]{1,0:T(8,128)} fusion(f32[16,256]{1,0:T(8,128)} %param.9, f32[256,128]{1,0:T(8,128)S(1)} %copy-done), kind=kOutput, calls=%fused_computation.48 | convolution fusion | flops 6291456 | bytes 155648 | tf_op jit(solution)/shard_map/dot_general | solution.py:65
  3.0 3.0 %collective-permute-start = (f32[16,128]{1,0:T(8,128)}, f32[16,128]{1,0:T(8,128)}, u32[]{:S(2)}, u32[]{:S(2)}) collective-permute-start(f32[16,128]{1,0:T(8,128)} %fusion.26), channel_id=1, source_target_pairs={{0,1},{1,0},{2,3},{3,2},{4,5},{5,4},{6,7},{7,6},{8,9},{9,8},{10,11... | collective-permute-start | bytes 24584 | tf_op jit(solution)/shard_map/ppermute | solution.py:69
  6.0 10.2 %all_gather.20 = f32[1024,128]{1,0:T(8,128)S(1)} all-gather(f32[256,128]{1,0:T(8,128)S(1)} %copy-done.1), channel_id=1, replica_groups=mesh['wide'=8,'narrow'=4] {'narrow'}, dimensions={0}, use_global_device_ids=true | all-gather | bytes 655360 | tf_op jit(solution)/shard_map/all_gather | solution.py:44
  17.0 7.2 %all_gather.19 = f32[16,1024]{1,0:T(8,128)S(1)} all-gather(f32[16,256]{1,0:T(8,128)S(1)} %copy-done.2), channel_id=1, replica_groups=mesh['wide'=8,'narrow'=4] {'narrow'}, dimensions={1}, use_global_device_ids=true | all-gather | bytes 81920 | tf_op jit(solution)/shard_map/all_gather | solution.py:58
  24.3 0.6 gather_fusion.1
  24.9 0.9 multiply_reduce_fusion
  27.3 15.2 %all_gather.22 = f32[1024,128]{1,0:T(8,128)S(1)} all-gather(f32[128,128]{1,0:T(8,128)S(1)} %copy-done.4), channel_id=1, replica_groups=mesh['wide'=8,'narrow'=4] {'wide'}, dimensions={0}, use_global_device_ids=true | all-gather | bytes 589824 | tf_op jit(solution)/shard_map/all_gather | solution.py:79
  42.7 1.1 %fusion.2 = f32[256,1024]{1,0:T(8,128)S(1)} fusion(f32[256,128]{1,0:T(8,128)S(1)} %copy-done.1, f32[1024,128]{1,0:T(8,128)S(1)} %all_gather.22, f32[1024]{0:T(1024)S(1)} %multiply_reduce_fusion.1, f32[256]{0:T(256)S(1)} %multiply_reduce_fusion.2), kind=kOutput, calls=%fused_computation.6 | convolution fusion | flops 403701760 | bytes 1709056 | tf_op jit(solution)/shard_map/while/body/eval_jaxpr/dot_general | solution.py:15
  43.9 0.6 copy-done.8
  44.5 1.2 %fusion.7 = f32[2,8,128,128]{2,3,1,0:T(8,128)S(1)} fusion(f32[2,8,128,128]{3,2,1,0:T(8,128)S(1)} %bitcast.65, f32[2,128,128,1]{2,1,3,0:T(8,128)S(1)} %bitcast.67, f32[2,8]{1,0:T(2,128)S(1)} %copy-done.9, f32[2,8,128]{2,1,0:T(8,128)S(1)} %copy-done.5, f32[2,128]{1,0:T(2,128)S(1)} %bitcast.70), kind=kOutput, calls=%fused_computation.12 | convolution fusion | flops 403963904 | bytes 2237504 | tf_op jit(solution)/shard_map/ipd,ikqd->ikpq/dot_general | solution.py:46
  45.8 0.6 convolution_bitcast_fusion.1
  46.4 0.7 add.98
  47.1 1.7 %collective-permute-start.1 = (f32[16,128]{1,0:T(8,128)S(1)}, f32[16,128]{1,0:T(8,128)S(1)}, u32[]{:S(2)}, u32[]{:S(2)}) collective-permute-start(f32[16,128]{1,0:T(8,128)S(1)} %add.98), channel_id=1, source_target_pairs={{0,2},{1,3},{2,0},{3,1},{4,6},{5,7},{6,4},{7,5},{8,10},{9,11},{10,... | collective-permute-start | bytes 24584 | tf_op jit(solution)/shard_map/ppermute | solution.py:69
  48.8 1.9 %collective-permute-done.1 = f32[16,128]{1,0:T(8,128)S(1)} collective-permute-done((f32[16,128]{1,0:T(8,128)S(1)}, f32[16,128]{1,0:T(8,128)S(1)}, u32[]{:S(2)}, u32[]{:S(2)}) %collective-permute-start.1) | collective-permute-done | bytes 8224 | tf_op jit(solution)/shard_map/ppermute | solution.py:69
  50.8 14.1 %all_gather.21 = f32[16,1024]{1,0:T(8,128)S(1)} all-gather(f32[16,128]{1,0:T(8,128)S(1)} %add.99), channel_id=1, replica_groups=mesh['wide'=8,'narrow'=4] {'wide'}, dimensions={1}, use_global_device_ids=true | all-gather | bytes 73728 | tf_op jit(solution)/shard_map/all_gather | solution.py:74
  64.9 0.9 fusion.13
  66.0 8.4 %all_gather.23 = f32[16,1024]{1,0:T(8,128)S(1)} all-gather(f32[16,256]{1,0:T(8,128)S(1)} %fusion.13), channel_id=1, replica_groups=mesh['wide'=8,'narrow'=4] {'narrow'}, dimensions={1}, use_global_device_ids=true | all-gather | bytes 81920 | tf_op jit(solution)/shard_map/all_gather | solution.py:58
  74.8 0.7 gather_fusion.2
  75.5 2.6 %collective-permute-done.2 = f32[16,128]{1,0:T(8,128)S(1)} collective-permute-done((f32[16,128]{1,0:T(8,128)S(1)}, f32[16,128]{1,0:T(8,128)S(1)}, u32[]{:S(2)}, u32[]{:S(2)}) %collective-permute-start.2) | collective-permute-done | bytes 8224 | tf_op jit(solution)/shard_map/ppermute | solution.py:69
  78.4 0.6 convolution_bitcast_fusion
  79.1 2.7 %collective-permute-done.3 = f32[16,128]{1,0:T(8,128)S(1)} collective-permute-done((f32[16,128]{1,0:T(8,128)S(1)}, f32[16,128]{1,0:T(8,128)S(1)}, u32[]{:S(2)}, u32[]{:S(2)}) %collective-permute-start.3) | collective-permute-done | bytes 8224 | tf_op jit(solution)/shard_map/ppermute | solution.py:69
  81.8 13.9 %all_gather.24 = f32[16,1024]{1,0:T(8,128)S(1)} all-gather(f32[16,128]{1,0:T(8,128)S(1)} %add.107), channel_id=1, replica_groups=mesh['wide'=8,'narrow'=4] {'wide'}, dimensions={1}, use_global_device_ids=true | all-gather | bytes 73728 | tf_op jit(solution)/shard_map/all_gather | solution.py:74
  95.7 1.5 %multiply_add_fusion = (f32[16,256]{1,0:T(8,128)}, f32[16,256]{1,0:T(8,128)}) fusion(f32[16,256]{1,0:T(8,128)S(1)} %fusion.13, f32[16,256]{1,0:T(8,128)S(1)} %copy-done.3, f32[256,1024]{1,0:T(8,128)S(1)} %fusion.2, f32[16,1024]{1,0:T(8,128)S(1)} %all_gather.24, pred[1024]{0:T(1024)(128)(4,1)S(1)} %fusion.20, f32[2,2,8,128]{3,2,1,0:T(8,128)S(1)} %convolution_bitcast_fusion), kind=kOutput, calls=%fused_computation.34 | convolution fusion | flops 50368512 | bytes 1197056 | tf_op jit(solution)/shard_map/while/body/eval_jaxpr/rs,ps->rp/dot_general | solution.py:29
  (39 shorter events, 3.4 us)
Async XLA Ops:
  0.6 0.9 copy-start
  0.6 5.4 %copy-start.1 = (f32[256,128]{1,0:T(8,128)S(1)}, f32[256,128]{1,0:T(8,128)}, u32[]{:S(2)}) copy-start(f32[256,128]{1,0:T(8,128)} %param.7) | copy-start | bytes 393220
  3.0 43.4 %collective-permute-start = (f32[16,128]{1,0:T(8,128)}, f32[16,128]{1,0:T(8,128)}, u32[]{:S(2)}, u32[]{:S(2)}) collective-permute-start(f32[16,128]{1,0:T(8,128)} %fusion.26), channel_id=1, source_target_pairs={{0,1},{1,0},{2,3},{3,2},{4,5},{5,4},{6,7},{7,6},{8,9},{9,8},{10,11... | collective-permute-start | bytes 24584 | tf_op jit(solution)/shard_map/ppermute | solution.py:69
  16.3 0.7 copy-start.2
  17.0 25.7 %copy-start.7 = (f32[256]{0:T(256)}, f32[256]{0:T(256)S(1)}, u32[]{:S(2)}) copy-start(f32[256]{0:T(256)S(1)} %multiply_reduce_fusion.2) | copy-start | bytes 3076
  17.0 7.2 %copy-start.10 = (s32[2,8]{1,0:T(2,128)S(1)}, s32[2,8]{1,0:T(2,128)}, u32[]{:S(2)}) copy-start(s32[2,8]{1,0:T(2,128)} %param.12) | copy-start | bytes 196
  24.3 2.2 %copy-start.6 = (s32[1024]{0:T(1024)}, s32[1024]{0:T(1024)S(1)}, u32[]{:S(2)}) copy-start(s32[1024]{0:T(1024)S(1)} %pad_clamp_fusion) | copy-start | bytes 12292
  24.9 1.0 copy-start.11
  26.5 0.8 copy-start.4
  42.7 1.2 %copy-start.5 = (f32[2,8,128]{2,1,0:T(8,128)S(1)}, f32[2,8,128]{2,1,0:T(8,128)}, u32[]{:S(2)}) copy-start(f32[2,8,128]{2,1,0:T(8,128)} %multiply_reduce_fusion) | copy-start | bytes 24580
  42.7 1.2 %copy-start.9 = (f32[2,8]{1,0:T(2,128)S(1)}, f32[2,8]{1,0:T(2,128)}, u32[]{:S(2)}) copy-start(f32[2,8]{1,0:T(2,128)} %compare_convert_fusion) | copy-start | bytes 196
  43.9 0.7 copy-start.8
  47.1 3.7 %collective-permute-start.1 = (f32[16,128]{1,0:T(8,128)S(1)}, f32[16,128]{1,0:T(8,128)S(1)}, u32[]{:S(2)}, u32[]{:S(2)}) collective-permute-start(f32[16,128]{1,0:T(8,128)S(1)} %add.98), channel_id=1, source_target_pairs={{0,2},{1,3},{2,0},{3,1},{4,6},{5,7},{6,4},{7,5},{8,10},{9,11},{10,... | collective-permute-start | bytes 24584 | tf_op jit(solution)/shard_map/ppermute | solution.py:69
  50.8 14.1 %copy-start.3 = (f32[16,256]{1,0:T(8,128)S(1)}, f32[16,256]{1,0:T(8,128)}, u32[]{:S(2)}) copy-start(f32[16,256]{1,0:T(8,128)} %param.8) | copy-start | bytes 49156
  74.4 3.7 %collective-permute-start.2 = (f32[16,128]{1,0:T(8,128)S(1)}, f32[16,128]{1,0:T(8,128)S(1)}, u32[]{:S(2)}, u32[]{:S(2)}) collective-permute-start(f32[16,128]{1,0:T(8,128)S(1)} %fusion.27), channel_id=1, source_target_pairs={{0,1},{1,0},{2,3},{3,2},{4,5},{5,4},{6,7},{7,6},{8,9},{9,8},{10,11... | collective-permute-start | bytes 24584 | tf_op jit(solution)/shard_map/ppermute | solution.py:69
  78.1 3.7 %collective-permute-start.3 = (f32[16,128]{1,0:T(8,128)S(1)}, f32[16,128]{1,0:T(8,128)S(1)}, u32[]{:S(2)}, u32[]{:S(2)}) collective-permute-start(f32[16,128]{1,0:T(8,128)S(1)} %add.106), channel_id=1, source_target_pairs={{0,2},{1,3},{2,0},{3,1},{4,6},{5,7},{6,4},{7,5},{8,10},{9,11},{10,... | collective-permute-start | bytes 24584 | tf_op jit(solution)/shard_map/ppermute | solution.py:69
